TPU v7x, 32 devices: a whole 2x2x4 slice. The times are simulated.
32 devices in a mesh: expert: 4 (over y, x), dp: 8 (over z, core).
Axes of the slice: x: 2, y: 2, z: 4, core: 2. Of those that a mesh axis runs over, the one named last changes fastest.
Arguments:
- x_new: bfloat16 [128, 4096], P('expert', 'dp'), may hold values from -6 to 6
- routes_new: int32 [128, 2], P('expert'), may hold values from 0 to 3, all different within a row; in each aligned block of 32 rows (0 to 31, 32 to 63, ...) at most 32 rows name the same one
- gates_new: float32 [128, 2], P('expert'), may hold values from 0.2 to 1
- w_gate: bfloat16 [4, 4096, 7168], P('expert', None, 'dp'), may hold values from -0.09375 to 0.09375
- w_up: bfloat16 [4, 4096, 7168], P('expert', None, 'dp'), may hold values from -0.09375 to 0.09375
- w_down: bfloat16 [4, 7168, 4096], P('expert', 'dp'), may hold values from -0.09375 to 0.09375
- grad_out: bfloat16 [256, 4096], P('expert', 'dp'), may hold values from -6 to 6
- routes_old: int32 [256, 2], P('expert'), may hold values from 0 to 3, all different within a row; in each aligned block of 64 rows (0 to 63, 64 to 127, ...) at most 64 rows name the same one
- gates_old: float32 [256, 2], P('expert'), may hold values from 0.2 to 1
- pre_gate: bfloat16 [4, 256, 7168], P('expert', None, 'dp'), may hold values from -8 to 8
- pre_up: bfloat16 [4, 256, 7168], P('expert', None, 'dp'), may hold values from -6 to 6
Outputs:
- mixed: bfloat16 [128, 4096], P('expert', 'dp')
- grad_down: bfloat16 [4, 7168, 4096], P('expert', 'dp')
- grad_gate: bfloat16 [4, 256, 7168], P('expert', None, 'dp')
- grad_up: bfloat16 [4, 256, 7168], P('expert', None, 'dp')
Inputs may be any that keep to these rules, and one draw needn't show every extreme that they name: `routes_new`: in each group of 32 tokens each expert is named by at most 32 tokens, and by exactly 32 tokens in some group; the two experts of a token differ. `routes_old`: in each group of 64 tokens each expert is named by at most 64 tokens, and by exactly 64 tokens in some group; the two experts of a token differ.
All inputs are finite; a program needn't handle non-finite values.
Results may differ from a plain program's by a relative error of at most 0.0078.
Values may be sent and summed in bfloat16 or wider, within the bound.
A program may use at most 64 MiB of HBM per device.

v0:
```python
import functools

import jax
import jax.numpy as jnp
from jax import lax
from jax.experimental import pallas as pl
from jax.experimental.pallas import tpu as pltpu
from jax.sharding import PartitionSpec as P

CAP_B = 32
CAP_A = 64


def slot_table(routes, capacity, experts):
    pairs = routes.reshape(-1)
    onehot = (pairs[:, None] == jnp.arange(experts, dtype=jnp.int32)[None, :]).astype(jnp.int32)
    before = jnp.cumsum(onehot, axis=0) - onehot
    slot = jnp.sum(before * onehot, axis=1)
    column = pairs * capacity + slot
    table = (jnp.arange(experts * capacity, dtype=jnp.int32)[:, None] == column[None, :]).astype(
        jnp.float32
    )
    return table.reshape(experts * capacity, routes.shape[0], 2)


def per_device(
    x_new,
    routes_new,
    gates_new,
    w_gate,
    w_up,
    w_down,
    grad_out,
    routes_old,
    gates_old,
    pre_gate,
    pre_up,
):
    experts = lax.axis_size("expert")
    slice_width = x_new.shape[1]
    gate_weight = w_gate[0]
    up_weight = w_up[0]
    down_weight = w_down[0]
    rows_new = experts * CAP_B
    rows_old = experts * CAP_A
    table_new = slot_table(routes_new, CAP_B, experts)
    picks = jnp.sum(table_new, axis=2).astype(jnp.bfloat16)
    outgoing = jnp.dot(picks, x_new, preferred_element_type=jnp.float32).astype(jnp.bfloat16)
    arrived = lax.all_to_all(
        outgoing.reshape(experts, CAP_B, slice_width),
        "expert",
        split_axis=0,
        concat_axis=0,
        tiled=True,
    )
    arrived = arrived.reshape(rows_new, slice_width)
    piece = lax.all_gather(arrived, "dp", axis=1, tiled=True)
    gate_pre = jnp.dot(piece, gate_weight, preferred_element_type=jnp.float32)
    up_pre = jnp.dot(piece, up_weight, preferred_element_type=jnp.float32)
    hidden = (jax.nn.silu(gate_pre) * up_pre).astype(jnp.bfloat16)
    partial_value = jnp.dot(hidden, down_weight, preferred_element_type=jnp.float32)
    result = lax.psum_scatter(partial_value, "dp", scatter_dimension=1, tiled=True).astype(
        jnp.bfloat16
    )
    returned = lax.all_to_all(
        result.reshape(experts, CAP_B, slice_width),
        "expert",
        split_axis=0,
        concat_axis=0,
        tiled=True,
    )
    returned = returned.reshape(rows_new, slice_width)
    weights_new = jnp.sum(table_new * gates_new[None, :, :], axis=2)
    mixed = jnp.dot(
        weights_new.T, returned.astype(jnp.float32), precision=lax.Precision.HIGHEST
    ).astype(jnp.bfloat16)
    table_old = slot_table(routes_old, CAP_A, experts)
    weights_old = jnp.sum(table_old * gates_old[None, :, :], axis=2)
    cotangent = jnp.dot(
        weights_old, grad_out.astype(jnp.float32), precision=lax.Precision.HIGHEST
    ).astype(jnp.bfloat16)
    landed = lax.all_to_all(
        cotangent.reshape(experts, CAP_A, slice_width),
        "expert",
        split_axis=0,
        concat_axis=0,
        tiled=True,
    )
    landed = landed.reshape(rows_old, slice_width)
    saved_gate = pre_gate[0].astype(jnp.float32)
    saved_up = pre_up[0].astype(jnp.float32)
    sigma = jax.nn.sigmoid(saved_gate)
    active = saved_gate * sigma
    hidden_old = (active * saved_up).astype(jnp.bfloat16)
    piece = lax.all_gather(landed, "dp", axis=1, tiled=True)
    grad_hidden = lax.dot_general(
        piece, down_weight, (((1,), (1,)), ((), ())), preferred_element_type=jnp.float32
    )
    block = lax.dot_general(
        hidden_old, piece, (((0,), (0,)), ((), ())), preferred_element_type=jnp.float32
    )
    weight_grad = block
    grad_hidden, weight_grad = (grad_hidden, weight_grad)
    gate_grad = (grad_hidden * saved_up * sigma * (1.0 + saved_gate * (1.0 - sigma))).astype(
        jnp.bfloat16
    )
    up_grad = (grad_hidden * active).astype(jnp.bfloat16)
    return (mixed, weight_grad.astype(jnp.bfloat16)[None], gate_grad[None], up_grad[None])


MESH = pl.DeviceIdType.MESH
F32 = jnp.float32
BF16 = jnp.bfloat16


def exchange_kernel(
    ne,
    nz,
    x_hbm,
    g_hbm,
    ro_hbm,
    go_hbm,
    rn_hbm,
    gn_hbm,
    pg_hbm,
    pu_hbm,
    wg_hbm,
    wu_hbm,
    wd_hbm,
    mixed_ref,
    gate_ref,
    up_ref,
    hid_ref,
    cot_ref,
    xg,
    gg,
    ro_all,
    go_all,
    rn_all,
    gn_all,
    pg_ref,
    pu_ref,
    wg,
    wu,
    wd,
    factor,
    active,
    hsum,
    usum,
    hnew,
    psend,
    precv,
    pown,
    rsend,
    rrecv,
    zsend,
    zrecv,
    wsem,
    lsem,
    ms,
    mr,
    x1s,
    x1r,
    x2s,
    x2r,
    x3s,
    x3r,
    g1s,
    g1r,
    g2s,
    g2r,
    g3s,
    g3r,
    ps,
    pr,
    rs,
    rr,
    zs,
    zr,
):
    e = lax.axis_index("expert")
    d = lax.axis_index("dp")
    z = d // 2
    c = d % 2
    other = z * 2 + 1 - c
    tb, width = x_hbm.shape
    ta = g_hbm.shape[0]
    hidden = wg.shape[2]

    def zat(j):
        return lax.rem(z + nz - j, nz)

    def rows(i, size):
        return pl.ds(pl.multiple_of(i * size, size), size)

    def peer(k):
        return lax.rem(e + k, ne)

    def remote(src, dst, ssem, rsem, to):
        return pltpu.make_async_remote_copy(
            src_ref=src, dst_ref=dst, send_sem=ssem, recv_sem=rsem, device_id=to, device_id_type=MESH
        )

    def block(buf, slot, size):
        return buf.at[slot, rows(e, size)]

    def first(buf, size, s, r, k):
        to = lax.rem(z + k, nz) * 2 + c
        return remote(block(buf, d, size), block(buf, d, size), s.at[k - 1], r.at[k - 1], (e, to))

    col, row = e % 2, e // 2
    sides = (row * 2 + 1 - col, (1 - row) * 2 + col)
    corner = (1 - row) * 2 + 1 - col

    def second(buf, size, s, r, j, k):
        place = block(buf, zat(j) * 2 + c, size)
        i = j * 4 + k
        return remote(place, place, s.at[i], r.at[i], (sides[k], d))

    def second_in(buf, size, s, r, j, k):
        place = buf.at[zat(j) * 2 + c, rows(sides[k], size)]
        return remote(place, place, s.at[j * 4 + k], r.at[j * 4 + k], (sides[k], d))

    def half(buf, who, size, j, k):
        start = pl.multiple_of(who * size + k * (size // 2), size // 2)
        return buf.at[zat(j) * 2 + c, pl.ds(start, size // 2)]

    def relay(buf, size, s, r, j, k):
        place = half(buf, sides[k], size, j, k)
        i = j * 4 + 2 + k
        return remote(place, place, s.at[i], r.at[i], (sides[1 - k], d))

    def relay_in(buf, size, s, r, j, k):
        place = half(buf, corner, size, j, k)
        i = j * 4 + 2 + k
        return remote(place, place, s.at[i], r.at[i], (sides[1 - k], d))

    def pass_on(buf, size, s, r, j):
        for k in range(2):
            second_in(buf, size, s, r, j, k).wait_recv()
            relay(buf, size, s, r, j, k).start()

    def third(buf, s, r, j):
        slot = zat(j) * 2 + c
        return remote(buf.at[slot], buf.at[slot], s.at[j], r.at[j], (e, other))

    def third_in(buf, s, r, j):
        slot = zat(j) * 2 + 1 - c
        return remote(buf.at[slot], buf.at[slot], s.at[j], r.at[j], (e, other))

    def first_in(buf, size, s, r, j):
        slot = zat(j) * 2 + c
        place = block(buf, slot, size)
        return remote(place, place, s.at[j - 1], r.at[j - 1], (e, slot))

    def order(i):
        return zat(lax.rem(i, nz)) * 2 + jnp.where(i < nz, c, 1 - c)

    def load_in(i):
        slot = order(i)
        part = rows(slot, width)
        return (
            pltpu.make_async_copy(wg_hbm.at[0, part], wg.at[slot], wsem.at[0, i]),
            pltpu.make_async_copy(wu_hbm.at[0, part], wu.at[slot], wsem.at[1, i]),
        )

    def load_down(i):
        slot = order(i)
        return pltpu.make_async_copy(wd_hbm.at[0, :, rows(slot, width)], wd.at[slot], wsem.at[2, i])

    own_x = pltpu.make_async_copy(x_hbm, block(xg, d, tb), lsem.at[0])
    own_g = pltpu.make_async_copy(g_hbm, block(gg, d, ta), lsem.at[1])
    own_a = pltpu.make_async_copy(pg_hbm, pg_ref, lsem.at[2])
    own_b = pltpu.make_async_copy(pu_hbm, pu_ref, lsem.at[3])
    notes = ((ro_hbm, ro_all), (go_hbm, go_all), (rn_hbm, rn_all), (gn_hbm, gn_all))
    own_notes = [
        pltpu.make_async_copy(own, there.at[e], lsem.at[4 + n]) for n, (own, there) in enumerate(notes)
    ]
    own_x.start()
    own_g.start()
    for load in own_notes:
        load.start()

    barrier = pltpu.get_barrier_semaphore()
    friends = [(peer(k), d) for k in range(1, ne)]
    friends += [(e, lax.rem(z + k, nz) * 2 + c) for k in range(1, nz)]
    friends += [(e, other)]
    for to in friends:
        pl.semaphore_signal(barrier, inc=1, device_id=to, device_id_type=MESH)
    own_a.start()
    own_b.start()

    @pl.loop(0, 2 * nz)
    def _(i):
        for load in load_in(i):
            load.start()

    @pl.loop(0, 2 * nz)
    def _(i):
        load_down(i).start()

    own_x.wait()
    own_g.wait()
    for load in own_notes:
        load.wait()
    pl.semaphore_wait(barrier, len(friends))

    def note_to(n, k):
        there = notes[n][1].at[e]
        i = n * (ne - 1) + k - 1
        return remote(there, there, ms.at[i], mr.at[i], (peer(k), d))

    def note_in(n, k):
        place = notes[n][1].at[lax.rem(e + ne - k, ne)]
        i = n * (ne - 1) + k - 1
        return remote(place, place, ms.at[i], mr.at[i], (peer(k), d))

    for k in range(1, nz):
        first(xg, tb, x1s, x1r, k).start()
    for k in range(2):
        second(xg, tb, x2s, x2r, 0, k).start()
    for n in range(4):
        for k in range(1, ne):
            note_to(n, k).start()
    for k in range(1, nz):
        first(gg, ta, g1s, g1r, k).start()

    step = 32
    wide = 128
    own_a.wait()
    own_b.wait()

    @pl.loop(0, pg_ref.shape[0] // wide)
    def _(i):
        r = rows(i, wide)
        v = pg_ref[r].astype(F32)
        u = pu_ref[r].astype(F32)
        s = jax.nn.sigmoid(v)
        a = v * s
        active[r] = a
        factor[r] = u * s * (1.0 + v * (1.0 - s))
        hid_ref[:, r] = (a * u).T.astype(BF16)

    for j in range(1, nz):
        first_in(xg, tb, x1s, x1r, j).wait_recv()
        for k in range(2):
            second(xg, tb, x2s, x2r, j, k).start()
    pass_on(xg, tb, x2s, x2r, 0)
    pass_on(xg, tb, x2s, x2r, 1)
    for k in range(2):
        second(gg, ta, g2s, g2r, 0, k).start()
    for j in range(2, nz):
        pass_on(xg, tb, x2s, x2r, j)
    for j in range(1, nz):
        first_in(gg, ta, g1s, g1r, j).wait_recv()
        for k in range(2):
            second(gg, ta, g2s, g2r, j, k).start()

    for n in range(4):
        for k in range(1, ne):
            note_in(n, k).wait_recv()

    def joined(there):
        return jnp.concatenate([there[g] for g in range(ne)], axis=1)

    mine = e
    routes_a, routes_b = joined(ro_all), joined(rn_all)
    all_a, all_b = joined(go_all), joined(gn_all)
    hit0 = routes_a[0:1] == mine
    hit1 = routes_a[1:2] == mine
    gates_a = jnp.where(hit0, all_a[0:1], 0.0) + jnp.where(hit1, all_a[1:2], 0.0)
    named = jnp.where(hit0 | hit1, 1.0, 0.0)
    na = named.shape[1]
    ri = lax.broadcasted_iota(jnp.int32, (na, na), 0)
    ci = lax.broadcasted_iota(jnp.int32, (na, na), 1)
    base = ci // ta * ta
    earlier = jnp.where((ri < ci) & (ri >= base), 1.0, 0.0).astype(BF16)
    before = jnp.dot(
        jnp.broadcast_to(named, (16, na)).astype(BF16), earlier, preferred_element_type=F32
    )[0:1]
    target = jnp.where(named > 0.5, before, -1.0 * na)
    chosen = (ri - base).astype(F32) == target
    pick_a = jnp.where(chosen, 1.0, 0.0).astype(BF16)
    row_gate = jnp.sum(jnp.where(chosen, gates_a, 0.0), axis=1, keepdims=True)
    nb = ne * tb
    gates_b = jnp.where(routes_b[0:1] == mine, all_b[0:1], 0.0) + jnp.where(
        routes_b[1:2] == mine, all_b[1:2], 0.0
    )
    rb = lax.broadcasted_iota(jnp.int32, (nb, nb), 0)
    cb = lax.broadcasted_iota(jnp.int32, (nb, nb), 1)
    row_b = jnp.sum(jnp.where(rb == cb, gates_b, 0.0), axis=1, keepdims=True)

    hsum[...] = jnp.zeros_like(hsum)
    usum[...] = jnp.zeros_like(usum)

    def project(i):
        slot = order(i)
        for load in load_in(i):
            load.wait()
        piece = xg[slot]
        hsum[...] += jnp.dot(piece, wg[slot], preferred_element_type=F32)
        usum[...] += jnp.dot(piece, wu[slot], preferred_element_type=F32)

    @pl.loop(0, nz)
    def _(i):
        for k in range(2):
            relay_in(xg, tb, x2s, x2r, i, k).wait_recv()
        third(xg, x3s, x3r, i).start()
        project(i)

    @pl.loop(0, nz)
    def _(i):
        third_in(xg, x3s, x3r, i).wait_recv()
        project(i + nz)

    @pl.loop(0, nb // step)
    def _(i):
        r = rows(i, step)
        v = hsum[r]
        hnew[r] = (v * jax.nn.sigmoid(v) * usum[r]).astype(BF16)

    def to_other(j):
        return remote(psend.at[j], precv.at[j], ps.at[j], pr.at[j], (e, other))

    @pl.loop(0, nz)
    def _(i):
        j = lax.rem(i + 1, nz)
        load_down(j + nz).wait()
        out = jnp.dot(hnew[...], wd[zat(j) * 2 + 1 - c], preferred_element_type=F32)
        psend[j] = (out * row_b).astype(BF16)
        to_other(j).start()
        load_down(j).wait()
        out = jnp.dot(hnew[...], wd[zat(j) * 2 + c], preferred_element_type=F32)
        pown[j] = out * row_b
        pass_on(gg, ta, g2s, g2r, i)

    def to_group(j, k):
        i = j * (ne - 1) + k - 1
        return remote(
            rsend.at[j, rows(peer(k), tb)], rrecv.at[i], rs.at[i], rr.at[i], (peer(k), d)
        )

    turns = [j % nz for j in range(1, nz + 1)]
    for j in turns:
        to_other(j).wait_recv()
        total = pown[j] + precv[j].astype(F32)
        pown[j] = total
        rsend[j] = total.astype(BF16)
        for k in range(1, ne):
            to_group(j, k).start()

    for j in range(nz):
        for k in range(2):
            relay_in(gg, ta, g2s, g2r, j, k).wait_recv()
        third(gg, g3s, g3r, j).start()

    factor_sum = jnp.zeros((na, pg_ref.shape[1]), F32)

    def spread(slot):
        moved = jnp.dot(pick_a, gg[slot], preferred_element_type=F32)
        cot = (moved * row_gate).astype(BF16)
        cot_ref[:, rows(slot, width)] = cot

    @pl.loop(0, nz)
    def _(i):
        spread(zat(i) * 2 + c)

    def to_depth(j):
        return remote(zsend.at[j - 1], zrecv.at[j - 1], zs.at[j - 1], zr.at[j - 1], (e, zat(j) * 2 + c))

    kept = None
    for j in turns:
        for k in range(1, ne):
            to_group(j, k).wait_recv()
        total = pown[j, rows(e, tb)]
        for k in range(1, ne):
            total = total + rrecv[j * (ne - 1) + k - 1].astype(F32)
        if j:
            zsend[j - 1] = total.astype(BF16)
            to_depth(j).start()
        else:
            kept = total

    @pl.loop(0, nz)
    def _(i):
        third_in(gg, g3s, g3r, i).wait_recv()
        spread(zat(i) * 2 + 1 - c)

    def back(i, total):
        return total + lax.dot_general(
            cot_ref[:, rows(i, width)],
            wd[i],
            (((1,), (1,)), ((), ())),
            preferred_element_type=F32,
        )

    grad = lax.fori_loop(0, 2 * nz, back, factor_sum)
    gate_ref[...] = (grad * factor[...]).astype(BF16)
    up_ref[...] = (grad * active[...]).astype(BF16)

    for j in range(1, nz):
        to_depth(j).wait_recv()
        kept = kept + zrecv[j - 1].astype(F32)
    mixed_ref[...] = kept.astype(BF16)

    for k in range(1, nz):
        first(xg, tb, x1s, x1r, k).wait_send()
        first(gg, ta, g1s, g1r, k).wait_send()
        to_depth(k).wait_send()
    for n in range(4):
        for k in range(1, ne):
            note_to(n, k).wait_send()
    for j in range(nz):
        for k in range(1, ne):
            to_group(j, k).wait_send()
        for k in range(2):
            second(xg, tb, x2s, x2r, j, k).wait_send()
            second(gg, ta, g2s, g2r, j, k).wait_send()
            relay(xg, tb, x2s, x2r, j, k).wait_send()
            relay(gg, ta, g2s, g2r, j, k).wait_send()
        third(xg, x3s, x3r, j).wait_send()
        third(gg, g3s, g3r, j).wait_send()
        to_other(j).wait_send()


def outer_kernel(hid_ref, cot_ref, m_ref, g_ref, u_ref, m_out, g_out, u_out, out_ref, sem):
    pairs = ((m_ref, m_out), (g_ref, g_out), (u_ref, u_out))
    copies = [pltpu.make_async_copy(src, dst, sem.at[n]) for n, (src, dst) in enumerate(pairs)]

    @pl.when(pl.program_id(0) == 0)
    def _():
        for copy in copies:
            copy.start()

    size = hid_ref.shape[0] // 2
    for i in range(2):
        part = pl.ds(i * size, size)
        out_ref[part] = jnp.dot(hid_ref[part], cot_ref[...], preferred_element_type=F32).astype(BF16)

    @pl.when(pl.program_id(0) == pl.num_programs(0) - 1)
    def _():
        for copy in copies:
            copy.wait()


def per_device_fused(
    x_new,
    routes_new,
    gates_new,
    w_gate,
    w_up,
    w_down,
    grad_out,
    routes_old,
    gates_old,
    pre_gate,
    pre_up,
):
    ne = lax.axis_size("expert")
    ndp = lax.axis_size("dp")
    nz = ndp // 2
    tb, width = x_new.shape
    ta = grad_out.shape[0]
    hidden = w_gate.shape[2]
    na, nb = ne * ta, ne * tb
    vmem = pl.BlockSpec(memory_space=pltpu.VMEM)
    hbm = pl.BlockSpec(memory_space=pltpu.HBM)

    def pair(count):
        return [pltpu.SemaphoreType.DMA((count,)), pltpu.SemaphoreType.DMA((count,))]

    gather_sems = pair(nz - 1) + pair(nz * 4) + pair(nz)
    mixed, gate_grad, up_grad, hidden_old, cotangent = pl.pallas_call(
        functools.partial(exchange_kernel, ne, nz),
        out_shape=(
            jax.ShapeDtypeStruct((tb, width), BF16),
            jax.ShapeDtypeStruct((na, hidden), BF16),
            jax.ShapeDtypeStruct((na, hidden), BF16),
            jax.ShapeDtypeStruct((hidden, na), BF16),
            jax.ShapeDtypeStruct((na, ndp * width), BF16),
        ),
        in_specs=[hbm] * 11,
        out_specs=(vmem,) * 5,
        scratch_shapes=[
            pltpu.VMEM((ndp, nb, width), BF16),
            pltpu.VMEM((ndp, na, width), BF16),
            pltpu.VMEM((ne, 2, ta), jnp.int32),
            pltpu.VMEM((ne, 2, ta), F32),
            pltpu.VMEM((ne, 2, tb), jnp.int32),
            pltpu.VMEM((ne, 2, tb), F32),
            pltpu.VMEM((na, hidden), BF16),
            pltpu.VMEM((na, hidden), BF16),
            pltpu.VMEM((ndp, width, hidden), BF16),
            pltpu.VMEM((ndp, width, hidden), BF16),
            pltpu.VMEM((ndp, hidden, width), BF16),
            pltpu.VMEM((na, hidden), F32),
            pltpu.VMEM((na, hidden), F32),
            pltpu.VMEM((nb, hidden), F32),
            pltpu.VMEM((nb, hidden), F32),
            pltpu.VMEM((nb, hidden), BF16),
            pltpu.VMEM((nz, nb, width), BF16),
            pltpu.VMEM((nz, nb, width), BF16),
            pltpu.VMEM((nz, nb, width), F32),
            pltpu.VMEM((nz, nb, width), BF16),
            pltpu.VMEM((nz * (ne - 1), tb, width), BF16),
            pltpu.VMEM((nz - 1, tb, width), BF16),
            pltpu.VMEM((nz - 1, tb, width), BF16),
            pltpu.SemaphoreType.DMA((3, ndp)),
            pltpu.SemaphoreType.DMA((8,)),
        ]
        + pair(4 * (ne - 1))
        + gather_sems
        + gather_sems
        + pair(nz)
        + pair(nz * (ne - 1))
        + pair(nz - 1),
        compiler_params=pltpu.CompilerParams(
            collective_id=0, has_side_effects=True, vmem_limit_bytes=42 * 1024 * 1024
        ),
        name="exchange",
    )(
        *(
            pltpu.with_memory_space_constraint(value, pltpu.HBM)
            for value in (
                x_new,
                grad_out,
                routes_old.T,
                gates_old.T,
                routes_new.T,
                gates_new.T,
                pre_gate[0],
                pre_up[0],
                w_gate,
                w_up,
                w_down,
            )
        )
    )
    mixed, gate_grad, up_grad, weight_grad = pl.pallas_call(
        outer_kernel,
        out_shape=tuple(
            jax.ShapeDtypeStruct(like.shape, BF16) for like in (mixed, gate_grad, up_grad)
        )
        + (jax.ShapeDtypeStruct((hidden, ndp * width), BF16),),
        grid=(ndp,),
        in_specs=[
            pl.BlockSpec((hidden, na), lambda i: (0, 0)),
            pl.BlockSpec((na, width), lambda i: (0, i)),
            vmem,
            vmem,
            vmem,
        ],
        out_specs=(hbm, hbm, hbm, pl.BlockSpec((hidden, width), lambda i: (0, i))),
        scratch_shapes=[pltpu.SemaphoreType.DMA((3,))],
        compiler_params=pltpu.CompilerParams(vmem_limit_bytes=16 * 1024 * 1024),
        cost_estimate=pl.CostEstimate(
            flops=2 * hidden * na * ndp * width,
            bytes_accessed=2 * (hidden * na + na * ndp * width + hidden * ndp * width),
            transcendentals=0,
        ),
        name="outer",
    )(hidden_old, cotangent, mixed, gate_grad, up_grad)
    return (mixed, weight_grad[None], gate_grad[None], up_grad[None])


def pick_body(mesh):
    ne, ndp = mesh.shape["expert"], mesh.shape["dp"]

    def body(*args):
        x_new, w_gate = args[0], args[3]
        whole_tiles = x_new.shape[1] % 128 == 0 and w_gate.shape[2] % 128 == 0
        full_slots = x_new.shape[0] == CAP_B and args[6].shape[0] == CAP_A
        if ndp % 2 == 0 and ndp > 2 and ne == 4 and whole_tiles and full_slots:
            return per_device_fused(*args)
        return per_device(*args)

    return body


def solution(mesh):
    body = pick_body(mesh)
    placed = (
        P("expert", "dp"),
        P("expert", None),
        P("expert", None),
        P("expert", None, "dp"),
        P("expert", None, "dp"),
        P("expert", "dp", None),
        P("expert", "dp"),
        P("expert", None),
        P("expert", None),
        P("expert", None, "dp"),
        P("expert", None, "dp"),
    )
    return jax.shard_map(
        body,
        mesh=mesh,
        in_specs=placed,
        out_specs=(
            P("expert", "dp"),
            P("expert", "dp", None),
            P("expert", None, "dp"),
            P("expert", None, "dp"),
        ),
        check_vma=False,
    )
```

profile of v0, /device:TPU:0, one launch (start us, length us, event | category | flops | bytes accessed | tf_op | source)
XLA Modules:
  0.0 46.0 jit_solution(5790469330733258019)
XLA Ops:
  0.6 39.5 %exchange.1 = (bf16[32,512]{1,0:T(8,128)(2,1)S(1)}, bf16[256,896]{1,0:T(8,128)(2,1)S(1)}, bf16[256,896]{1,0:T(8,128)(2,1)S(1)}, bf16[896,256]{1,0:T(8,128)(2,1)S(1)}, bf16[256,4096]{1,0:T(8,128)(2,1)S(1)}) custom-call(bf16[32,512]{1,0:T(8,128)(2,1)} %x_hbm.1, bf16[64,512]{1,0:T(8,128)(2,1)} %g_hbm.1, s32[2,64]{1,0:T(2,128)} %bitcast.11, f32[2,64]{1,0:T(2,128)} %bitcast.12, ...), custom_call_target="tpu_custom_call" | custom-call | tf_op jit(solution)/shard_map/exchange/pallas_call | solution.py:573
  40.2 5.9 %outer.1 = (bf16[32,512]{1,0:T(8,128)(2,1)}, bf16[256,896]{1,0:T(8,128)(2,1)}, bf16[256,896]{1,0:T(8,128)(2,1)}, bf16[896,4096]{1,0:T(8,128)(2,1)}) custom-call(bf16[896,256]{1,0:T(8,128)(2,1)S(1)} %get-tuple-element.13.hid_ref, bf16[256,4096]{1,0:T(8,128)(2,1)S(1)} %get-tuple-element.14.cot_ref, bf16[32,512]{1,0:T(8,128)(2,1)S(1)} %get-tuple-element.15.m_ref, ...), custom_call_target="tpu_custom_call" | custom-call | flops 1879048192 | bytes 9895936 | tf_op jit(solution)/shard_map/outer/pallas_call | solution.py:639
where the time goes:
time: 46.2 us; the launch traced here: 46 us
  Pallas kernels  45.4 us (98%)
  between operations  0.64 us (1%)
    pallas_call x1, Pallas kernels, per_device_fused(): pl.pallas_call(functools.partial(exchange_kernel, ne, nz), out_shape=(jax...  39.5 us
    pallas_call x1, Pallas kernels, per_device_fused(): pl.pallas_call(outer_kernel, out_shape=tuple((jax.ShapeDtypeStruct(like.s...  5.88 us

commit v1 on v0

--- a/solution.py
+++ b/solution.py
@@ -128,10 +128,11 @@
     wu_hbm,
     wd_hbm,
     mixed_ref,
-    gate_ref,
-    up_ref,
-    hid_ref,
+    out_ref,
     cot_ref,
+    wd,
+    factor,
+    active,
     xg,
     gg,
     ro_all,
@@ -142,12 +143,12 @@
     pu_ref,
     wg,
     wu,
-    wd,
-    factor,
-    active,
     hsum,
     usum,
     hnew,
+    hid_ref,
+    pick_ref,
+    gate_rows,
     psend,
     precv,
     pown,
@@ -187,8 +188,15 @@
     ta = g_hbm.shape[0]
     hidden = wg.shape[2]
 
-    def zat(j):
-        return lax.rem(z + nz - j, nz)
+    inner = jnp.minimum(z, nz - 1 - z)
+    outward = jnp.where(z < nz - 1 - z, 1, -1)
+
+    def near(j):
+        beside = jnp.where(j % 2 == 1, -((j + 1) // 2), j // 2)
+        return z + jnp.where(j <= 2 * inner, beside, outward * (j - inner))
+
+    def back_by(j):
+        return lax.rem(z + nz - near(j), nz)
 
     def rows(i, size):
         return pl.ds(pl.multiple_of(i * size, size), size)
@@ -213,17 +221,17 @@
     corner = (1 - row) * 2 + 1 - col
 
     def second(buf, size, s, r, j, k):
-        place = block(buf, zat(j) * 2 + c, size)
+        place = block(buf, near(j) * 2 + c, size)
         i = j * 4 + k
         return remote(place, place, s.at[i], r.at[i], (sides[k], d))
 
     def second_in(buf, size, s, r, j, k):
-        place = buf.at[zat(j) * 2 + c, rows(sides[k], size)]
+        place = buf.at[near(j) * 2 + c, rows(sides[k], size)]
         return remote(place, place, s.at[j * 4 + k], r.at[j * 4 + k], (sides[k], d))
 
     def half(buf, who, size, j, k):
         start = pl.multiple_of(who * size + k * (size // 2), size // 2)
-        return buf.at[zat(j) * 2 + c, pl.ds(start, size // 2)]
+        return buf.at[near(j) * 2 + c, pl.ds(start, size // 2)]
 
     def relay(buf, size, s, r, j, k):
         place = half(buf, sides[k], size, j, k)
@@ -241,32 +249,34 @@
             relay(buf, size, s, r, j, k).start()
 
     def third(buf, s, r, j):
-        slot = zat(j) * 2 + c
+        slot = near(j) * 2 + c
         return remote(buf.at[slot], buf.at[slot], s.at[j], r.at[j], (e, other))
 
     def third_in(buf, s, r, j):
-        slot = zat(j) * 2 + 1 - c
+        slot = near(j) * 2 + 1 - c
         return remote(buf.at[slot], buf.at[slot], s.at[j], r.at[j], (e, other))
 
     def first_in(buf, size, s, r, j):
-        slot = zat(j) * 2 + c
+        slot = near(j) * 2 + c
         place = block(buf, slot, size)
-        return remote(place, place, s.at[j - 1], r.at[j - 1], (e, slot))
+        i = back_by(j) - 1
+        return remote(place, place, s.at[i], r.at[i], (e, slot))
 
     def order(i):
-        return zat(lax.rem(i, nz)) * 2 + jnp.where(i < nz, c, 1 - c)
-
-    def load_in(i):
-        slot = order(i)
+        return near(i % nz) * 2 + jnp.where(i < nz, c, 1 - c)
+
+    def load_in(slot):
         part = rows(slot, width)
         return (
-            pltpu.make_async_copy(wg_hbm.at[0, part], wg.at[slot], wsem.at[0, i]),
-            pltpu.make_async_copy(wu_hbm.at[0, part], wu.at[slot], wsem.at[1, i]),
+            pltpu.make_async_copy(wg_hbm.at[0, part], wg.at[slot], wsem.at[0, slot]),
+            pltpu.make_async_copy(wu_hbm.at[0, part], wu.at[slot], wsem.at[1, slot]),
         )
 
-    def load_down(i):
-        slot = order(i)
-        return pltpu.make_async_copy(wd_hbm.at[0, :, rows(slot, width)], wd.at[slot], wsem.at[2, i])
+    def load_down(slot):
+        return pltpu.make_async_copy(wd_hbm.at[0, :, rows(slot, width)], wd.at[slot], wsem.at[2, slot])
+
+    def from_own(i):
+        return lax.rem(d + i, 2 * nz)
 
     own_x = pltpu.make_async_copy(x_hbm, block(xg, d, tb), lsem.at[0])
     own_g = pltpu.make_async_copy(g_hbm, block(gg, d, ta), lsem.at[1])
@@ -292,12 +302,12 @@
 
     @pl.loop(0, 2 * nz)
     def _(i):
-        for load in load_in(i):
+        for load in load_in(from_own(i)):
             load.start()
 
     @pl.loop(0, 2 * nz)
     def _(i):
-        load_down(i).start()
+        load_down(from_own(i)).start()
 
     own_x.wait()
     own_g.wait()
@@ -315,15 +325,15 @@
         i = n * (ne - 1) + k - 1
         return remote(place, place, ms.at[i], mr.at[i], (peer(k), d))
 
-    for k in range(1, nz):
-        first(xg, tb, x1s, x1r, k).start()
+    for j in range(1, nz):
+        first(xg, tb, x1s, x1r, nz - back_by(j)).start()
     for k in range(2):
         second(xg, tb, x2s, x2r, 0, k).start()
     for n in range(4):
         for k in range(1, ne):
             note_to(n, k).start()
-    for k in range(1, nz):
-        first(gg, ta, g1s, g1r, k).start()
+    for k in range(2):
+        second(gg, ta, g2s, g2r, 0, k).start()
 
     step = 32
     wide = 128
@@ -341,20 +351,13 @@
         factor[r] = u * s * (1.0 + v * (1.0 - s))
         hid_ref[:, r] = (a * u).T.astype(BF16)
 
+    pass_on(xg, tb, x2s, x2r, 0)
+    for j in range(1, nz):
+        first(gg, ta, g1s, g1r, nz - back_by(j)).start()
     for j in range(1, nz):
         first_in(xg, tb, x1s, x1r, j).wait_recv()
         for k in range(2):
             second(xg, tb, x2s, x2r, j, k).start()
-    pass_on(xg, tb, x2s, x2r, 0)
-    pass_on(xg, tb, x2s, x2r, 1)
-    for k in range(2):
-        second(gg, ta, g2s, g2r, 0, k).start()
-    for j in range(2, nz):
-        pass_on(xg, tb, x2s, x2r, j)
-    for j in range(1, nz):
-        first_in(gg, ta, g1s, g1r, j).wait_recv()
-        for k in range(2):
-            second(gg, ta, g2s, g2r, j, k).start()
 
     for n in range(4):
         for k in range(1, ne):
@@ -380,8 +383,10 @@
     )[0:1]
     target = jnp.where(named > 0.5, before, -1.0 * na)
     chosen = (ri - base).astype(F32) == target
-    pick_a = jnp.where(chosen, 1.0, 0.0).astype(BF16)
-    row_gate = jnp.sum(jnp.where(chosen, gates_a, 0.0), axis=1, keepdims=True)
+    pick_ref[...] = jnp.where(chosen, 1.0, 0.0).astype(BF16)
+    gate_rows[...] = jnp.broadcast_to(
+        jnp.sum(jnp.where(chosen, gates_a, 0.0), axis=1, keepdims=True), gate_rows.shape
+    )
     nb = ne * tb
     gates_b = jnp.where(routes_b[0:1] == mine, all_b[0:1], 0.0) + jnp.where(
         routes_b[1:2] == mine, all_b[1:2], 0.0
@@ -389,29 +394,68 @@
     rb = lax.broadcasted_iota(jnp.int32, (nb, nb), 0)
     cb = lax.broadcasted_iota(jnp.int32, (nb, nb), 1)
     row_b = jnp.sum(jnp.where(rb == cb, gates_b, 0.0), axis=1, keepdims=True)
-
     hsum[...] = jnp.zeros_like(hsum)
     usum[...] = jnp.zeros_like(usum)
 
-    def project(i):
-        slot = order(i)
-        for load in load_in(i):
-            load.wait()
-        piece = xg[slot]
-        hsum[...] += jnp.dot(piece, wg[slot], preferred_element_type=F32)
-        usum[...] += jnp.dot(piece, wu[slot], preferred_element_type=F32)
-
-    @pl.loop(0, nz)
-    def _(i):
+    for j in range(1, nz):
+        pass_on(xg, tb, x2s, x2r, j)
+        if j == nz - 2:
+            pass_on(gg, ta, g2s, g2r, 0)
+
+    def project(*steps):
+        slots = [order(i) for i in steps]
+        for slot in slots:
+            for load in load_in(slot):
+                load.wait()
+        for total, w in ((hsum, wg), (usum, wu)):
+            parts = [jnp.dot(xg[slot], w[slot], preferred_element_type=F32) for slot in slots]
+            total[...] += sum(parts[1:], parts[0])
+
+    def collect(i):
         for k in range(2):
             relay_in(xg, tb, x2s, x2r, i, k).wait_recv()
         third(xg, x3s, x3r, i).start()
-        project(i)
-
-    @pl.loop(0, nz)
+
+    def spread_plane(j):
+        first_in(gg, ta, g1s, g1r, j).wait_recv()
+        for k in range(2):
+            second(gg, ta, g2s, g2r, j, k).start()
+
+    def arrive(j):
+        for k in range(2):
+            relay_in(gg, ta, g2s, g2r, j, k).wait_recv()
+        third(gg, g3s, g3r, j).start()
+
+    spread_plane(1)
+
+    collect(0)
+    collect(1)
+    project(0, 1)
+    for j in range(2, nz - 1):
+        spread_plane(j)
+
+    @pl.loop(2, nz)
     def _(i):
-        third_in(xg, x3s, x3r, i).wait_recv()
-        project(i + nz)
+        collect(i)
+
+        @pl.when(i == 2)
+        def _():
+            arrive(0)
+
+        third_in(xg, x3s, x3r, i - 2).wait_recv()
+        project(i, i - 2 + nz)
+
+        @pl.when(i == 2)
+        def _():
+            spread_plane(nz - 1)
+            pass_on(gg, ta, g2s, g2r, 1)
+
+    third_in(xg, x3s, x3r, nz - 2).wait_recv()
+    third_in(xg, x3s, x3r, nz - 1).wait_recv()
+    project(2 * nz - 2, 2 * nz - 1)
+
+    for j in range(2, nz - 1):
+        pass_on(gg, ta, g2s, g2r, j)
 
     @pl.loop(0, nb // step)
     def _(i):
@@ -422,26 +466,13 @@
     def to_other(j):
         return remote(psend.at[j], precv.at[j], ps.at[j], pr.at[j], (e, other))
 
-    @pl.loop(0, nz)
-    def _(i):
-        j = lax.rem(i + 1, nz)
-        load_down(j + nz).wait()
-        out = jnp.dot(hnew[...], wd[zat(j) * 2 + 1 - c], preferred_element_type=F32)
-        psend[j] = (out * row_b).astype(BF16)
-        to_other(j).start()
-        load_down(j).wait()
-        out = jnp.dot(hnew[...], wd[zat(j) * 2 + c], preferred_element_type=F32)
-        pown[j] = out * row_b
-        pass_on(gg, ta, g2s, g2r, i)
-
     def to_group(j, k):
         i = j * (ne - 1) + k - 1
         return remote(
             rsend.at[j, rows(peer(k), tb)], rrecv.at[i], rs.at[i], rr.at[i], (peer(k), d)
         )
 
-    turns = [j % nz for j in range(1, nz + 1)]
-    for j in turns:
+    def pair_sum(j):
         to_other(j).wait_recv()
         total = pown[j] + precv[j].astype(F32)
         pown[j] = total
@@ -449,54 +480,88 @@
         for k in range(1, ne):
             to_group(j, k).start()
 
-    for j in range(nz):
-        for k in range(2):
-            relay_in(gg, ta, g2s, g2r, j, k).wait_recv()
-        third(gg, g3s, g3r, j).start()
-
-    factor_sum = jnp.zeros((na, pg_ref.shape[1]), F32)
-
-    def spread(slot):
-        moved = jnp.dot(pick_a, gg[slot], preferred_element_type=F32)
-        cot = (moved * row_gate).astype(BF16)
-        cot_ref[:, rows(slot, width)] = cot
-
-    @pl.loop(0, nz)
+    group = 2 if nz % 2 == 0 else 1
+
+    @pl.loop(0, nz // group)
     def _(i):
-        spread(zat(i) * 2 + c)
+        planes = [nz - 1 - i * group - n for n in range(group)]
+        for j in planes:
+            for k in range(2):
+                load_down(near(j) * 2 + k).wait()
+        for j in planes:
+            out = jnp.dot(hnew[...], wd[near(j) * 2 + 1 - c], preferred_element_type=F32)
+            psend[j] = (out * row_b).astype(BF16)
+            out = jnp.dot(hnew[...], wd[near(j) * 2 + c], preferred_element_type=F32)
+            pown[j] = out * row_b
+        for j in planes:
+            to_other(j).start()
+
+        @pl.when(i == 0)
+        def _():
+            arrive(1)
+            pass_on(gg, ta, g2s, g2r, nz - 1)
 
     def to_depth(j):
-        return remote(zsend.at[j - 1], zrecv.at[j - 1], zs.at[j - 1], zr.at[j - 1], (e, zat(j) * 2 + c))
-
-    kept = None
-    for j in turns:
+        to = lax.rem(z + nz - j, nz) * 2 + c
+        return remote(zsend.at[j - 1], zrecv.at[j - 1], zs.at[j - 1], zr.at[j - 1], (e, to))
+
+    def group_sum(j):
         for k in range(1, ne):
             to_group(j, k).wait_recv()
         total = pown[j, rows(e, tb)]
         for k in range(1, ne):
             total = total + rrecv[j * (ne - 1) + k - 1].astype(F32)
-        if j:
-            zsend[j - 1] = total.astype(BF16)
-            to_depth(j).start()
-        else:
-            kept = total
-
-    @pl.loop(0, nz)
+        return total
+
+    def send_depth(j):
+        i = back_by(j)
+        zsend[i - 1] = group_sum(j).astype(BF16)
+        to_depth(i).start()
+
+    def spread(j):
+        for n in range(2):
+            moved = jnp.dot(pick_ref[...], gg[near(j) * 2 + n], preferred_element_type=F32)
+            for m in range(width // wide):
+                start = near(j) * 2 * width + n * width + m * wide
+                cot_ref[:, pl.ds(pl.multiple_of(start, wide), wide)] = (
+                    moved[:, m * wide : (m + 1) * wide] * gate_rows[...]
+                ).astype(BF16)
+
+    def outer(j):
+        cols = rows(near(j), 2 * width)
+        size = hidden // 2
+        for n in range(2):
+            part = pl.ds(n * size, size)
+            out_ref[part, cols] = jnp.dot(
+                hid_ref[part], cot_ref[:, cols], preferred_element_type=F32
+            ).astype(BF16)
+
+    third_in(gg, g3s, g3r, 0).wait_recv()
+    spread(0)
+    for j in range(nz - 1, nz // 2 - 1, -1):
+        pair_sum(j)
+    @pl.loop(1, nz)
     def _(i):
         third_in(gg, g3s, g3r, i).wait_recv()
-        spread(zat(i) * 2 + 1 - c)
-
-    def back(i, total):
-        return total + lax.dot_general(
-            cot_ref[:, rows(i, width)],
-            wd[i],
-            (((1,), (1,)), ((), ())),
-            preferred_element_type=F32,
-        )
-
-    grad = lax.fori_loop(0, 2 * nz, back, factor_sum)
-    gate_ref[...] = (grad * factor[...]).astype(BF16)
-    up_ref[...] = (grad * active[...]).astype(BF16)
+        outer(i - 1)
+        spread(i)
+        @pl.when(i == 1)
+        def _():
+            for j in range(nz // 2 - 1, -1, -1):
+                pair_sum(j)
+
+        @pl.when(i + 1 < nz)
+        def _():
+            arrive(i + 1)
+
+        @pl.when(i == nz - 2)
+        def _():
+            send_depth(nz - 1)
+
+    for j in range(nz - 2, 0, -1):
+        send_depth(j)
+    outer(nz - 1)
+    kept = group_sum(0)
 
     for j in range(1, nz):
         to_depth(j).wait_recv()
@@ -523,24 +588,55 @@
         to_other(j).wait_send()
 
 
-def outer_kernel(hid_ref, cot_ref, m_ref, g_ref, u_ref, m_out, g_out, u_out, out_ref, sem):
-    pairs = ((m_ref, m_out), (g_ref, g_out), (u_ref, u_out))
+def write_kernel(
+    pieces,
+    m_ref,
+    w_ref,
+    cot_ref,
+    wd,
+    factor,
+    active,
+    m_out,
+    g_out,
+    u_out,
+    w_out,
+    grad_ref,
+    g_ref,
+    u_ref,
+    sem,
+    gsem,
+):
+    size = w_ref.shape[0] // pieces
+    pairs = [(w_ref.at[pl.ds(n * size, size)], w_out.at[pl.ds(n * size, size)]) for n in range(pieces)]
+    pairs += [(m_ref, m_out)]
     copies = [pltpu.make_async_copy(src, dst, sem.at[n]) for n, (src, dst) in enumerate(pairs)]
-
-    @pl.when(pl.program_id(0) == 0)
-    def _():
-        for copy in copies:
-            copy.start()
-
-    size = hid_ref.shape[0] // 2
-    for i in range(2):
-        part = pl.ds(i * size, size)
-        out_ref[part] = jnp.dot(hid_ref[part], cot_ref[...], preferred_element_type=F32).astype(BF16)
-
-    @pl.when(pl.program_id(0) == pl.num_programs(0) - 1)
-    def _():
-        for copy in copies:
-            copy.wait()
+    for copy in copies:
+        copy.start()
+    half = wd.shape[1] // 2
+    width = wd.shape[2]
+    for m in range(2):
+        part = pl.ds(m * half, half)
+        parts = [
+            lax.dot_general(
+                wd[i, part],
+                cot_ref[:, pl.ds(i * width, width)],
+                (((1,), (1,)), ((), ())),
+                preferred_element_type=F32,
+            )
+            for i in range(wd.shape[0])
+        ]
+        grad_ref[part] = sum(parts[1:], parts[0])
+    wide = 128
+    for i in range(grad_ref.shape[0] // wide):
+        r = pl.ds(i * wide, wide)
+        grad = grad_ref[r].T
+        g_ref[:, r] = (grad * factor[:, r]).astype(BF16)
+        u_ref[:, r] = (grad * active[:, r]).astype(BF16)
+    last = [pltpu.make_async_copy(g_ref, g_out, gsem.at[0]), pltpu.make_async_copy(u_ref, u_out, gsem.at[1])]
+    for copy in last:
+        copy.start()
+    for copy in copies + last:
+        copy.wait()
 
 
 def per_device_fused(
@@ -570,17 +666,18 @@
         return [pltpu.SemaphoreType.DMA((count,)), pltpu.SemaphoreType.DMA((count,))]
 
     gather_sems = pair(nz - 1) + pair(nz * 4) + pair(nz)
-    mixed, gate_grad, up_grad, hidden_old, cotangent = pl.pallas_call(
+    mixed, weight_grad, *state = pl.pallas_call(
         functools.partial(exchange_kernel, ne, nz),
         out_shape=(
             jax.ShapeDtypeStruct((tb, width), BF16),
-            jax.ShapeDtypeStruct((na, hidden), BF16),
-            jax.ShapeDtypeStruct((na, hidden), BF16),
-            jax.ShapeDtypeStruct((hidden, na), BF16),
+            jax.ShapeDtypeStruct((hidden, ndp * width), BF16),
             jax.ShapeDtypeStruct((na, ndp * width), BF16),
+            jax.ShapeDtypeStruct((ndp, hidden, width), BF16),
+            jax.ShapeDtypeStruct((na, hidden), F32),
+            jax.ShapeDtypeStruct((na, hidden), F32),
         ),
         in_specs=[hbm] * 11,
-        out_specs=(vmem,) * 5,
+        out_specs=(vmem,) * 6,
         scratch_shapes=[
             pltpu.VMEM((ndp, nb, width), BF16),
             pltpu.VMEM((ndp, na, width), BF16),
@@ -592,12 +689,12 @@
             pltpu.VMEM((na, hidden), BF16),
             pltpu.VMEM((ndp, width, hidden), BF16),
             pltpu.VMEM((ndp, width, hidden), BF16),
-            pltpu.VMEM((ndp, hidden, width), BF16),
-            pltpu.VMEM((na, hidden), F32),
-            pltpu.VMEM((na, hidden), F32),
             pltpu.VMEM((nb, hidden), F32),
             pltpu.VMEM((nb, hidden), F32),
             pltpu.VMEM((nb, hidden), BF16),
+            pltpu.VMEM((hidden, na), BF16),
+            pltpu.VMEM((na, na), BF16),
+            pltpu.VMEM((na, 128), F32),
             pltpu.VMEM((nz, nb, width), BF16),
             pltpu.VMEM((nz, nb, width), BF16),
             pltpu.VMEM((nz, nb, width), F32),
@@ -615,7 +712,7 @@
         + pair(nz * (ne - 1))
         + pair(nz - 1),
         compiler_params=pltpu.CompilerParams(
-            collective_id=0, has_side_effects=True, vmem_limit_bytes=42 * 1024 * 1024
+            collective_id=0, has_side_effects=True, vmem_limit_bytes=34 * 1024 * 1024
         ),
         name="exchange",
     )(
@@ -636,30 +733,27 @@
             )
         )
     )
+    parts = next(n for n in (8, 7, 4, 2, 1) if hidden % (n * 16) == 0)
     mixed, gate_grad, up_grad, weight_grad = pl.pallas_call(
-        outer_kernel,
-        out_shape=tuple(
-            jax.ShapeDtypeStruct(like.shape, BF16) for like in (mixed, gate_grad, up_grad)
-        )
-        + (jax.ShapeDtypeStruct((hidden, ndp * width), BF16),),
-        grid=(ndp,),
-        in_specs=[
-            pl.BlockSpec((hidden, na), lambda i: (0, 0)),
-            pl.BlockSpec((na, width), lambda i: (0, i)),
-            vmem,
-            vmem,
-            vmem,
+        functools.partial(write_kernel, parts),
+        out_shape=(
+            jax.ShapeDtypeStruct((tb, width), BF16),
+            jax.ShapeDtypeStruct((na, hidden), BF16),
+            jax.ShapeDtypeStruct((na, hidden), BF16),
+            jax.ShapeDtypeStruct((hidden, ndp * width), BF16),
+        ),
+        in_specs=[vmem] * 6,
+        out_specs=(hbm,) * 4,
+        scratch_shapes=[
+            pltpu.VMEM((hidden, na), F32),
+            pltpu.VMEM((na, hidden), BF16),
+            pltpu.VMEM((na, hidden), BF16),
+            pltpu.SemaphoreType.DMA((parts + 1,)),
+            pltpu.SemaphoreType.DMA((2,)),
         ],
-        out_specs=(hbm, hbm, hbm, pl.BlockSpec((hidden, width), lambda i: (0, i))),
-        scratch_shapes=[pltpu.SemaphoreType.DMA((3,))],
-        compiler_params=pltpu.CompilerParams(vmem_limit_bytes=16 * 1024 * 1024),
-        cost_estimate=pl.CostEstimate(
-            flops=2 * hidden * na * ndp * width,
-            bytes_accessed=2 * (hidden * na + na * ndp * width + hidden * ndp * width),
-            transcendentals=0,
-        ),
-        name="outer",
-    )(hidden_old, cotangent, mixed, gate_grad, up_grad)
+        compiler_params=pltpu.CompilerParams(vmem_limit_bytes=8 * 1024 * 1024),
+        name="write",
+    )(mixed, weight_grad, *state)
     return (mixed, weight_grad[None], gate_grad[None], up_grad[None])
 
 

time: 46.2 us -> 38.9 us (0.84)
  Pallas kernels: 45.4 us -> 38.2 us
    pallas_call x1, Pallas kernels: 39.5 us -> 33.3 us  [per_device_fused(): pl.pallas_call(functools.partial(exchange_kernel, ne, nz), out_shape=(jax...]
    pallas_call x1, Pallas kernels: 5.88 us -> 4.83 us  [per_device_fused(): pl.pallas_call(functools.partial(write_kernel, parts), out_shape=(jax.Sha...]
where the time goes in v1:
time: 38.9 us; the launch traced here: 38.8 us
  Pallas kernels  38.2 us (98%)
  between operations  0.64 us (2%)
    pallas_call x1, Pallas kernels, per_device_fused(): pl.pallas_call(functools.partial(exchange_kernel, ne, nz), out_shape=(jax...  33.3 us
    pallas_call x1, Pallas kernels, per_device_fused(): pl.pallas_call(functools.partial(write_kernel, parts), out_shape=(jax.Sha...  4.83 us

profile of v1, /device:TPU:0, one launch (start us, length us, event | category | flops | bytes accessed | tf_op | source)
XLA Modules:
  0.0 38.8 jit_solution(2695507670929376013)
XLA Ops:
  0.6 33.3 %exchange.1 = (bf16[32,512]{1,0:T(8,128)(2,1)S(1)}, bf16[896,4096]{1,0:T(8,128)(2,1)S(1)}, bf16[256,4096]{1,0:T(8,128)(2,1)S(1)}, bf16[8,896,512]{2,1,0:T(8,128)...) custom-call(bf16[32,512]{1,0:T(8,128)(2,1)} %x_hbm.1, bf16[64,512]{1,0:T(8,128)(2,1)} %g_hbm.1, ...), custom_call_target="tpu_custom_call" | custom-call | tf_op jit(solution)/shard_map/exchange/pallas_call | solution.py:669
  34.0 4.8 %write.1 = (bf16[32,512]{1,0:T(8,128)(2,1)}, bf16[256,896]{1,0:T(8,128)(2,1)}, bf16[256,896]{1,0:T(8,128)(2,1)}, bf16[896,4096]{1,0:T(8,128)(2,1)}) custom-call(bf16[32,512]{1,0:T(8,128)(2,1)S(1)} %get-tuple-element.14.m_ref, bf16[896,4096]{1,0:T(8,128)(2,1)S(1)} %get-tuple-element.15.w_ref, bf16[256,4096]{1,0:T(8,128)(2,1)S(1)} %get-tuple-element.16.cot_ref, ...), custom_call_target="tpu_custom_call" | custom-call | tf_op jit(solution)/shard_map/write/pallas_call | solution.py:737
